TPU v7x, 256 devices: a whole 4x4x8 slice. The times are simulated.
256 devices in a mesh: dp: 32 (over z, y_lo, core), grp: 8 (over x, y_hi).
Axes of the slice: x: 4, y: 4 (y_hi: 2, y_lo: 2; y = y_hi * 2 + y_lo), z: 8, core: 2. Of those that a mesh axis runs over, the one named last changes fastest.
Arguments:
- acts: bfloat16 [131072, 1024], P(('dp', 'grp')), may hold values from -8 to 8, as said below
- grads: bfloat16 [131072, 1024], P(('dp', 'grp')), may hold values from -8 to 8, as said below
- damping: float32 [2], replicated, may hold values from 0.02 to 0.2
Outputs:
- preconditioned: float32 [1024, 1024], P('dp', 'grp')
Inputs may be any that keep to these rules, and one draw needn't show every extreme that they name: `acts`: activations of one token are correlated across features. `grads`: output gradients are correlated with the activations.
All inputs are finite; a program needn't handle non-finite values. Where the computation divides by a largest or mean magnitude, that divisor is 1e-20 or more.
Results may differ from a plain program's by a relative error of at most 0.0003.
Values sent between devices are 32-bit elements; how exact they have to be, the bound alone decides.
No kernel may reach another device: no remote copies, remote signals or barrier semaphores. Data moves between devices by JAX's collectives and lax.ppermute only.
A program may use at most 64 MiB of HBM per device.

v0:
```python
import jax
import jax.numpy as jnp
from jax import lax
from jax.sharding import Mesh
from jax.sharding import PartitionSpec as P

ITERS = 4
DP = ("dp_0", "dp_1", "dp_2")
DP_GRP = ("dp_0", "dp_1", "dp_2", "grp")


def in_blocks(array, dim, size):
    before, after = (array.shape[:dim], array.shape[dim + 1 :])
    return jnp.moveaxis(array.reshape(*before, size, -1, *after), dim, 0)


def sum_at_owner(array, axis, dim):
    pieces = in_blocks(array, dim, lax.axis_size(axis))
    arrived = lax.all_to_all(pieces, axis, split_axis=0, concat_axis=0, tiled=True)
    return arrived.sum(axis=0)


def copy_for_each(array, axis):
    size = lax.axis_size(axis)
    return lax.all_to_all(
        jnp.broadcast_to(array[None], (size, *array.shape)), axis, 0, 0, tiled=True
    )


def joined_along(pieces, dim):
    pieces = jnp.moveaxis(pieces, 0, dim)
    dims = pieces.shape
    return pieces.reshape(*dims[:dim], dims[dim] * dims[dim + 1], *dims[dim + 2 :])


def collect(array, axis, dim):
    pieces = copy_for_each(array, axis)
    return joined_along(pieces, dim)


def taken_together(array, axis):
    return copy_for_each(array, axis).max(axis=0)


def summed_rows_2(array, chips, core, dim):
    sizes = (lax.axis_size(chips), lax.axis_size(core))
    pieces = in_blocks(array, dim, sizes[0] * sizes[1])
    inside = pieces.shape[1:]
    pieces = pieces.reshape(*sizes, *inside).swapaxes(0, 1).reshape(-1, *inside)
    pieces = lax.psum_scatter(pieces, core, scatter_dimension=0, tiled=True)
    return lax.psum_scatter(pieces, chips, scatter_dimension=0, tiled=True)[0]


def batched(left, right):
    return jnp.einsum(
        "bij,bjk->bik",
        left,
        right,
        precision=lax.Precision.HIGHEST,
        preferred_element_type=jnp.float32,
    )


def local(acts, grads, damping):
    dp_size = lax.axis_size(DP)
    grp_size = lax.axis_size("grp")
    dp_index = lax.axis_index(DP)
    grp_index = lax.axis_index("grp")
    width = acts.shape[1]
    cols = width // grp_size
    rows = width // dp_size
    scale = 1.0 / (acts.shape[0] * dp_size * grp_size)
    contract = (((0,), (0,)), ((), ()))
    highest = lax.Precision.HIGHEST
    stacked = (
        jnp.stack(
            [
                lax.dot_general(acts, acts, contract, preferred_element_type=jnp.float32),
                lax.dot_general(grads, grads, contract, preferred_element_type=jnp.float32),
            ],
            axis=0,
        )
        * scale
    )
    row_sums = lax.psum_scatter(stacked, DP, scatter_dimension=1, tiled=True)
    block = sum_at_owner(row_sums, "grp", 2)
    row_start = dp_index * rows
    col_start = grp_index * cols
    row_ids = row_start + lax.broadcasted_iota(jnp.int32, (rows, cols), 0)
    col_ids = col_start + lax.broadcasted_iota(jnp.int32, (rows, cols), 1)
    diagonal = (row_ids == col_ids).astype(jnp.float32)
    matrix = block + damping[:, None, None] * diagonal[None]
    matrix_rows = collect(matrix, "grp", 2)
    largest = jnp.max(jnp.sum(jnp.abs(matrix_rows), axis=2), axis=1)
    bounds = taken_together(largest, DP)
    alpha = 1.0 / bounds
    iterate = alpha[:, None, None] * diagonal[None]
    for step in range(ITERS):
        columns = collect(iterate, DP, 1)
        image = batched(matrix_rows, columns)
        image_rows = collect(image, "grp", 2)
        update = batched(image_rows, columns)
        iterate = 2.0 * iterate - update
    inverse_cols = collect(iterate, DP, 1)
    inverses = lax.all_gather(inverse_cols, "grp", axis=2, tiled=True)
    mapped = jnp.dot(acts, inverses[0], precision=highest, preferred_element_type=jnp.float32)
    weighted = jnp.dot(grads, inverses[1], precision=highest, preferred_element_type=jnp.float32)
    summed_rows = summed_rows_2(
        lax.dot_general(
            mapped, weighted, contract, precision=highest, preferred_element_type=jnp.float32
        )
        * scale,
        ("dp_0", "dp_1"),
        "dp_2",
        0,
    )
    return sum_at_owner(summed_rows, "grp", 1)


def solution(mesh):
    torus = Mesh(mesh.devices.reshape(8, 2, 2, mesh.shape["grp"]), ("dp_0", "dp_1", "dp_2", "grp"))
    return jax.shard_map(
        local,
        mesh=torus,
        in_specs=(P(DP_GRP, None), P(DP_GRP, None), P()),
        out_specs=P(DP, "grp"),
        check_vma=False,
    )
```

profile of v0, /device:TPU:2, one launch (start us, length us, event | category | flops | bytes accessed | tf_op | source)
XLA Modules:
  0.0 666.9 jit_solution(8184046820750787442)
XLA Ops:
  6.5 2.9 convolution_bitcast_fusion
  9.5 1.3 convolution_bitcast_fusion.1
  10.8 4.2 maximum_multiply_fusion
  15.0 134.3 %reduce-scatter.4.cloned.1.call-done = f32[2,32,1024]{2,1,0:T(8,128)} async-done(((f32[2,1024,1024]{2,1,0:T(8,128)}), f32[2,32,1024]{2,1,0:T(8,128)}) %reduce-scatter.4.cloned.1.call-update) | async-done | bytes 262160 | tf_op jit(solution)/shard_map/reduce_scatter | solution.py:85
  149.3 1.7 bitcast_bitcast_fusion
  151.0 7.3 %all-to-all-start = ((f32[8,2,32,128]{3,2,1,0:T(8,128)}), f32[8,2,32,128]{3,2,1,0:T(8,128)S(1)}, u32[]{:S(2)}, u32[]{:S(2)}) async-start(f32[8,2,32,128]{3,2,1,0:T(8,128)} %bitcast_bitcast_fusion), calls=%async_computation.1 | async-start | bytes 524288 | tf_op jit(solution)/shard_map/all_to_all | solution.py:19
  158.4 6.6 all-to-all-done
  165.0 0.1 multiply_add_fusion
  165.1 11.3 %all_to_all.66 = f32[8,2,32,128]{3,2,1,0:T(8,128)S(1)} all-to-all(f32[8,2,32,128]{3,2,1,0:T(8,128)S(1)} %broadcast_in_dim.22), channel_id=1, replica_groups=mesh['dp_0'=8,'dp_1'=2,'dp_2'=2,'grp'=8] {'grp'}, dimensions={0} | all-to-all | bytes 524288 | tf_op jit(solution)/shard_map/all_to_all | solution.py:25
  176.5 0.1 fusion.18
  176.6 0.1 reduce_max.18
  176.7 12.9 %all_to_all.67 = f32[32,1,2]{2,1,0:T(1,128)S(1)} all-to-all(f32[32,1,2]{2,1,0:T(1,128)S(1)} %broadcast_in_dim.23), channel_id=1, replica_groups=mesh['dp_0'=8,'dp_1'=2,'dp_2'=2,'grp'=8] {'dp_0','dp_1','dp_2'}, dimensions={0} | all-to-all | bytes 512 | tf_op jit(solution)/shard_map/all_to_all | solution.py:25
  189.7 0.1 broadcast_in_dim.24
  189.9 32.2 %all_to_all.68 = f32[32,2,32,128]{3,2,1,0:T(8,128)S(1)} all-to-all(f32[32,2,32,128]{3,2,1,0:T(8,128)S(1)} %broadcast_in_dim.24), channel_id=1, replica_groups=mesh['dp_0'=8,'dp_1'=2,'dp_2'=2,'grp'=8] {'dp_0','dp_1','dp_2'}, dimensions={0} | all-to-all | bytes 2097152 | tf_op jit(solution)/shard_map/all_to_all | solution.py:25
  222.1 0.1 copy.34
  222.2 0.7 fusion.16
  222.9 11.3 %all_to_all.69 = f32[8,2,32,128]{3,2,1,0:T(8,128)S(1)} all-to-all(f32[8,2,32,128]{3,2,1,0:T(8,128)S(1)} %broadcast_in_dim.25), channel_id=1, replica_groups=mesh['dp_0'=8,'dp_1'=2,'dp_2'=2,'grp'=8] {'grp'}, dimensions={0} | all-to-all | bytes 524288 | tf_op jit(solution)/shard_map/all_to_all | solution.py:25
  234.2 0.7 convolution_subtract_fusion.3
  234.8 0.1 broadcast_in_dim.26
  235.0 31.6 %all_to_all.70 = f32[32,2,32,128]{3,2,1,0:T(8,128)S(1)} all-to-all(f32[32,2,32,128]{3,2,1,0:T(8,128)S(1)} %broadcast_in_dim.26), channel_id=1, replica_groups=mesh['dp_0'=8,'dp_1'=2,'dp_2'=2,'grp'=8] {'dp_0','dp_1','dp_2'}, dimensions={0} | all-to-all | bytes 2097152 | tf_op jit(solution)/shard_map/all_to_all | solution.py:25
  266.6 0.7 fusion.14
  267.3 12.2 %all_to_all.71 = f32[8,2,32,128]{3,2,1,0:T(8,128)S(1)} all-to-all(f32[8,2,32,128]{3,2,1,0:T(8,128)S(1)} %broadcast_in_dim.27), channel_id=1, replica_groups=mesh['dp_0'=8,'dp_1'=2,'dp_2'=2,'grp'=8] {'grp'}, dimensions={0} | all-to-all | bytes 524288 | tf_op jit(solution)/shard_map/all_to_all | solution.py:25
  279.6 0.7 convolution_subtract_fusion.2
  280.2 0.1 broadcast_in_dim.28
  280.4 31.6 %all_to_all.72 = f32[32,2,32,128]{3,2,1,0:T(8,128)S(1)} all-to-all(f32[32,2,32,128]{3,2,1,0:T(8,128)S(1)} %broadcast_in_dim.28), channel_id=1, replica_groups=mesh['dp_0'=8,'dp_1'=2,'dp_2'=2,'grp'=8] {'dp_0','dp_1','dp_2'}, dimensions={0} | all-to-all | bytes 2097152 | tf_op jit(solution)/shard_map/all_to_all | solution.py:25
  311.9 0.1 copy.38
  312.0 0.7 fusion.12
  312.7 12.0 %all_to_all.73 = f32[8,2,32,128]{3,2,1,0:T(8,128)S(1)} all-to-all(f32[8,2,32,128]{3,2,1,0:T(8,128)S(1)} %broadcast_in_dim.29), channel_id=1, replica_groups=mesh['dp_0'=8,'dp_1'=2,'dp_2'=2,'grp'=8] {'grp'}, dimensions={0} | all-to-all | bytes 524288 | tf_op jit(solution)/shard_map/all_to_all | solution.py:25
  324.7 0.7 convolution_subtract_fusion.1
  325.4 0.1 broadcast_in_dim.30
  325.5 31.6 %all_to_all.74 = f32[32,2,32,128]{3,2,1,0:T(8,128)S(1)} all-to-all(f32[32,2,32,128]{3,2,1,0:T(8,128)S(1)} %broadcast_in_dim.30), channel_id=1, replica_groups=mesh['dp_0'=8,'dp_1'=2,'dp_2'=2,'grp'=8] {'dp_0','dp_1','dp_2'}, dimensions={0} | all-to-all | bytes 2097152 | tf_op jit(solution)/shard_map/all_to_all | solution.py:25
  357.1 0.1 copy.40
  357.2 0.7 fusion.10
  357.9 12.1 %all_to_all.75 = f32[8,2,32,128]{3,2,1,0:T(8,128)S(1)} all-to-all(f32[8,2,32,128]{3,2,1,0:T(8,128)S(1)} %broadcast_in_dim.31), channel_id=1, replica_groups=mesh['dp_0'=8,'dp_1'=2,'dp_2'=2,'grp'=8] {'grp'}, dimensions={0} | all-to-all | bytes 524288 | tf_op jit(solution)/shard_map/all_to_all | solution.py:25
  370.0 0.7 convolution_subtract_fusion
  370.7 0.1 broadcast_in_dim.32
  370.8 31.7 %all_to_all.76 = f32[32,2,32,128]{3,2,1,0:T(8,128)S(1)} all-to-all(f32[32,2,32,128]{3,2,1,0:T(8,128)S(1)} %broadcast_in_dim.32), channel_id=1, replica_groups=mesh['dp_0'=8,'dp_1'=2,'dp_2'=2,'grp'=8] {'dp_0','dp_1','dp_2'}, dimensions={0} | all-to-all | bytes 2097152 | tf_op jit(solution)/shard_map/all_to_all | solution.py:25
  402.5 1.1 copy.42
  403.7 119.5 %all-gather.2.cloned.1.call-done = f32[2,1024,1024]{2,1,0:T(8,128)} async-done(((f32[2,1024,128]{2,1,0:T(8,128)}), f32[2,1024,1024]{2,1,0:T(8,128)}) %all-gather.2.cloned.1.call-update) | async-done | bytes 8388624 | tf_op jit(solution)/shard_map/all_gather | solution.py:105
  523.3 8.6 %fusion.1 = f32[1024,512]{1,0:T(8,128)S(1)} fusion(bf16[512,1024]{1,0:T(8,128)(2,1)S(1)} %copy-done, f32[2,1024,1024]{2,1,0:T(8,128)} %all-gather.2.cloned.1.call-done), kind=kOutput, calls=%fused_computation.4 | convolution fusion | flops 6442450944 | bytes 7340032 | tf_op jit(solution)/shard_map/dot_general | solution.py:106
  531.9 8.8 %fusion = f32[1024,512]{1,0:T(8,128)S(1)} fusion(bf16[512,1024]{1,0:T(8,128)(2,1)S(1)} %copy-done.1, f32[2,1024,1024]{2,1,0:T(8,128)} %all-gather.2.cloned.1.call-done), kind=kOutput, calls=%fused_computation.2 | convolution fusion | flops 6442450944 | bytes 7340032 | tf_op jit(solution)/shard_map/dot_general | solution.py:107
  540.7 6.9 %convolution_multiply_fusion = f32[1024,1024]{1,0:T(8,128)S(1)} fusion(f32[1024,512]{1,0:T(8,128)S(1)} %fusion.1, f32[1024,512]{1,0:T(8,128)S(1)} %fusion), kind=kOutput, calls=%fused_computation.5 | convolution fusion | flops 6443499520 | bytes 8388608 | tf_op jit(solution)/shard_map/dot_general | solution.py:109
  547.6 2.2 copy.43
  549.9 16.7 %reduce-scatter.6.cloned.1.call-done = f32[16,32,1024]{2,1,0:T(8,128)} async-done(((f32[32,32,1024]{2,1,0:T(8,128)}), f32[16,32,1024]{2,1,0:T(8,128)}) %reduce-scatter.6.cloned.1.call-update) | async-done | bytes 2097168 | tf_op jit(solution)/shard_map/reduce_scatter | solution.py:50
  566.6 79.0 %reduce-scatter.8.cloned.1.call-done = f32[1,32,1024]{2,1,0:T(8,128)} async-done(((f32[16,32,1024]{2,1,0:T(8,128)}), f32[1,32,1024]{2,1,0:T(8,128)}) %reduce-scatter.8.cloned.1.call-update) | async-done | bytes 131088 | tf_op jit(solution)/shard_map/reduce_scatter | solution.py:51
  645.6 0.9 copy.52
  646.5 13.2 %all_to_all.77 = f32[8,32,128]{2,1,0:T(8,128)S(1)} all-to-all(f32[8,32,128]{2,1,0:T(8,128)S(1)} %bitcast.128), channel_id=1, replica_groups=mesh['dp_0'=8,'dp_1'=2,'dp_2'=2,'grp'=8] {'grp'}, dimensions={0} | all-to-all | bytes 262144 | tf_op jit(solution)/shard_map/all_to_all | solution.py:19
  659.8 0.6 reduce_sum.29
  (29 shorter events, 0.6 us)
Async XLA Ops:
  6.5 2.9 copy-start
  6.5 142.8 %reduce-scatter.4.cloned.1.call-start = ((), (), s32[]{:S(2)}) async-start(), calls=%async_computation.16 | async-start | bytes 8650752 | tf_op jit(solution)/shard_map/reduce_scatter | solution.py:85
  15.0 150.1 %copy-start.2 = (f32[2]{0:T(128)S(1)}, f32[2]{0:T(128)}, u32[]{:S(2)}) copy-start(f32[2]{0:T(128)} %param.5) | copy-start | bytes 28
  151.0 14.0 %all-to-all-start = ((f32[8,2,32,128]{3,2,1,0:T(8,128)}), f32[8,2,32,128]{3,2,1,0:T(8,128)S(1)}, u32[]{:S(2)}, u32[]{:S(2)}) async-start(f32[8,2,32,128]{3,2,1,0:T(8,128)} %bitcast_bitcast_fusion), calls=%async_computation.1 | async-start | bytes 524288 | tf_op jit(solution)/shard_map/all_to_all | solution.py:19
  158.3 364.9 %all-gather.2.cloned.1.call-start = ((), (), s32[]{:S(2)}) async-start(), calls=%async_computation.17 | async-start | bytes 9437184 | tf_op jit(solution)/shard_map/all_gather | solution.py:105
  403.7 128.2 %copy-start.1 = (bf16[512,1024]{1,0:T(8,128)(2,1)S(1)}, bf16[512,1024]{1,0:T(8,128)(2,1)}, u32[]{:S(2)}) copy-start(bf16[512,1024]{1,0:T(8,128)(2,1)} %param.4) | copy-start | bytes 3145732
  403.7 162.9 %reduce-scatter.6.cloned.1.call-start = ((), (), s32[]{:S(2)}) async-start(), calls=%async_computation.18 | async-start | bytes 6291456 | tf_op jit(solution)/shard_map/reduce_scatter | solution.py:50
  549.8 95.8 %reduce-scatter.8.cloned.1.call-start = ((), (), s32[]{:S(2)}) async-start(), calls=%async_computation.19 | async-start | bytes 2228224 | tf_op jit(solution)/shard_map/reduce_scatter | solution.py:51
Sparse Core Ops, SparseCore 0:
  15.1 134.1 reduce-scatter.3
  403.8 119.4 all-gather.1
  549.9 16.5 reduce-scatter.5
  569.0 76.5 reduce-scatter.7
where the time goes:
time: 668 us; the launch traced here: 667 us
  waiting for transfers between devices  356 us (53%)
  blocking collectives  244 us (37%)
  matrix products  33.7 us (5%)
  between operations  13.4 us (2%)
  starting transfers between devices  7.41 us (1%)
  local copies, waits for them, and re-layouts  7.01 us (1%)
    all_to_all x11, blocking collectives, copy_for_each(): lax.all_to_all(jnp.broadcast_to(array[None], (size, *array.shape)), axis,...  231 us
    reduce_scatter x1, waiting for transfers between devices, local(): row_sums = lax.psum_scatter(stacked, DP, scatter_dimension=1, tiled=True)  134 us
    all_gather x1, waiting for transfers between devices, local(): inverses = lax.all_gather(inverse_cols, 'grp', axis=2, tiled=True)  120 us
    reduce_scatter x1, waiting for transfers between devices, summed_rows_2(): return lax.psum_scatter(pieces, chips, scatter_dimension=0, tiled=True)[0]  79 us
    reduce_scatter x1, waiting for transfers between devices, summed_rows_2(): pieces = lax.psum_scatter(pieces, core, scatter_dimension=0, tiled=True)  16.7 us
  transfers between devices with their start and end apart: 5, of which 5 were waited for; matrix products, arithmetic and copies ran while one was open for 0% of the time, Pallas kernels for 0%

commit v1 on v0

--- a/solution.py
+++ b/solution.py
@@ -1,12 +1,22 @@
+import functools
 import jax
 import jax.numpy as jnp
 from jax import lax
 from jax.sharding import Mesh
 from jax.sharding import PartitionSpec as P
+from jax.lax import all_to_all, psum
 
 ITERS = 4
 DP = ("dp_0", "dp_1", "dp_2")
 DP_GRP = ("dp_0", "dp_1", "dp_2", "grp")
+
+
+def begin_copies_on(sheet, device_axis):
+    local_now = jnp.stack([sheet] * psum(1, device_axis), axis=0)
+    return jnp.concatenate(all_to_all(local_now, device_axis, concat_axis=0, split_axis=0), axis=2)
+
+
+balance_steps_all = functools.partial(begin_copies_on, device_axis="grp")
 
 
 def in_blocks(array, dim, size):
@@ -102,7 +112,7 @@
         update = batched(image_rows, columns)
         iterate = 2.0 * iterate - update
     inverse_cols = collect(iterate, DP, 1)
-    inverses = lax.all_gather(inverse_cols, "grp", axis=2, tiled=True)
+    inverses = balance_steps_all(inverse_cols)
     mapped = jnp.dot(acts, inverses[0], precision=highest, preferred_element_type=jnp.float32)
     weighted = jnp.dot(grads, inverses[1], precision=highest, preferred_element_type=jnp.float32)
     summed_rows = summed_rows_2(

time: 668 us -> 637 us (0.954)
  waiting for transfers between devices: 356 us -> 232 us
  blocking collectives: 244 us -> 344 us
  matrix products: 33.7 us -> 23.5 us
    all_gather x1 -> x0, waiting for transfers between devices: 120 us -> none  [local(): inverses = lax.all_gather(inverse_cols, 'grp', axis=2, tiled=True)]
    all_to_all x0 -> x1, blocking collectives: none -> 99.9 us  [begin_copies_on(): all_to_all(local_now, device_axis, concat_axis=0, split_axis=0)]
  transfers between devices with their start and end apart: 5 -> 4, of which waited for: 5 -> 4; matrix products, arithmetic and copies ran while one was open for 0% -> 0% of each run, Pallas kernels for 0% -> 0%
where the time goes in v1:
time: 637 us; the launch traced here: 636 us
  blocking collectives  344 us (54%)
  waiting for transfers between devices  232 us (36%)
  matrix products  23.5 us (4%)
  between operations  13.4 us (2%)
  local copies, waits for them, and re-layouts  10.6 us (2%)
  starting transfers between devices  7.37 us (1%)
    all_to_all x11, blocking collectives, copy_for_each(): lax.all_to_all(jnp.broadcast_to(array[None], (size, *array.shape)), axis,...  231 us
    reduce_scatter x1, waiting for transfers between devices, local(): row_sums = lax.psum_scatter(stacked, DP, scatter_dimension=1, tiled=True)  134 us
    all_to_all x1, blocking collectives, begin_copies_on(): all_to_all(local_now, device_axis, concat_axis=0, split_axis=0)  99.9 us
    reduce_scatter x1, waiting for transfers between devices, summed_rows_2(): return lax.psum_scatter(pieces, chips, scatter_dimension=0, tiled=True)[0]  79.4 us
    all_to_all x1, blocking collectives, sum_at_owner(): lax.all_to_all(pieces, axis, split_axis=0, concat_axis=0, tiled=True)  13.1 us
  transfers between devices with their start and end apart: 4, of which 4 were waited for; matrix products, arithmetic and copies ran while one was open for 0% of the time, Pallas kernels for 0%

profile of v1, /device:TPU:2, one launch (start us, length us, event | category | flops | bytes accessed | tf_op | source)
XLA Modules:
  0.0 636.4 jit_solution(12402007356754987292)
XLA Ops:
  6.5 2.9 convolution_bitcast_fusion
  9.5 1.3 convolution_bitcast_fusion.1
  10.8 4.2 maximum_multiply_fusion
  15.0 134.3 %reduce-scatter.4.cloned.1.call-done = f32[2,32,1024]{2,1,0:T(8,128)} async-done(((f32[2,1024,1024]{2,1,0:T(8,128)}), f32[2,32,1024]{2,1,0:T(8,128)}) %reduce-scatter.4.cloned.1.call-update) | async-done | bytes 262160 | tf_op jit(solution)/shard_map/reduce_scatter | solution.py:95
  149.3 1.7 bitcast_bitcast_fusion
  151.0 7.3 %all-to-all-start = ((f32[8,2,32,128]{3,2,1,0:T(8,128)}), f32[8,2,32,128]{3,2,1,0:T(8,128)S(1)}, u32[]{:S(2)}, u32[]{:S(2)}) async-start(f32[8,2,32,128]{3,2,1,0:T(8,128)} %bitcast_bitcast_fusion), calls=%async_computation.1 | async-start | bytes 524288 | tf_op jit(solution)/shard_map/all_to_all | solution.py:29
  158.4 6.6 %all-to-all-done = f32[8,2,32,128]{3,2,1,0:T(8,128)S(1)} async-done(((f32[8,2,32,128]{3,2,1,0:T(8,128)}), f32[8,2,32,128]{3,2,1,0:T(8,128)S(1)}, u32[]{:S(2)}, u32[]{:S(2)}) %all-to-all-start) | async-done | bytes 262176 | tf_op jit(solution)/shard_map/all_to_all | solution.py:29
  165.0 0.1 multiply_add_fusion
  165.1 11.3 %all_to_all.71 = f32[8,2,32,128]{3,2,1,0:T(8,128)S(1)} all-to-all(f32[8,2,32,128]{3,2,1,0:T(8,128)S(1)} %broadcast_in_dim.22), channel_id=1, replica_groups=mesh['dp_0'=8,'dp_1'=2,'dp_2'=2,'grp'=8] {'grp'}, dimensions={0} | all-to-all | bytes 524288 | tf_op jit(solution)/shard_map/all_to_all | solution.py:35
  176.5 0.1 fusion.16
  176.6 0.1 reduce_max.18
  176.7 12.9 %all_to_all.72 = f32[32,1,2]{2,1,0:T(1,128)S(1)} all-to-all(f32[32,1,2]{2,1,0:T(1,128)S(1)} %broadcast_in_dim.23), channel_id=1, replica_groups=mesh['dp_0'=8,'dp_1'=2,'dp_2'=2,'grp'=8] {'dp_0','dp_1','dp_2'}, dimensions={0} | all-to-all | bytes 512 | tf_op jit(solution)/shard_map/all_to_all | solution.py:35
  189.7 0.1 broadcast_in_dim.24
  189.9 32.2 %all_to_all.73 = f32[32,2,32,128]{3,2,1,0:T(8,128)S(1)} all-to-all(f32[32,2,32,128]{3,2,1,0:T(8,128)S(1)} %broadcast_in_dim.24), channel_id=1, replica_groups=mesh['dp_0'=8,'dp_1'=2,'dp_2'=2,'grp'=8] {'dp_0','dp_1','dp_2'}, dimensions={0} | all-to-all | bytes 2097152 | tf_op jit(solution)/shard_map/all_to_all | solution.py:35
  222.2 0.7 fusion.14
  222.9 11.3 %all_to_all.74 = f32[8,2,32,128]{3,2,1,0:T(8,128)S(1)} all-to-all(f32[8,2,32,128]{3,2,1,0:T(8,128)S(1)} %broadcast_in_dim.25), channel_id=1, replica_groups=mesh['dp_0'=8,'dp_1'=2,'dp_2'=2,'grp'=8] {'grp'}, dimensions={0} | all-to-all | bytes 524288 | tf_op jit(solution)/shard_map/all_to_all | solution.py:35
  234.2 0.7 convolution_subtract_fusion.3
  234.8 0.1 broadcast_in_dim.26
  235.0 31.6 %all_to_all.75 = f32[32,2,32,128]{3,2,1,0:T(8,128)S(1)} all-to-all(f32[32,2,32,128]{3,2,1,0:T(8,128)S(1)} %broadcast_in_dim.26), channel_id=1, replica_groups=mesh['dp_0'=8,'dp_1'=2,'dp_2'=2,'grp'=8] {'dp_0','dp_1','dp_2'}, dimensions={0} | all-to-all | bytes 2097152 | tf_op jit(solution)/shard_map/all_to_all | solution.py:35
  266.6 0.7 fusion.12
  267.3 12.2 %all_to_all.76 = f32[8,2,32,128]{3,2,1,0:T(8,128)S(1)} all-to-all(f32[8,2,32,128]{3,2,1,0:T(8,128)S(1)} %broadcast_in_dim.27), channel_id=1, replica_groups=mesh['dp_0'=8,'dp_1'=2,'dp_2'=2,'grp'=8] {'grp'}, dimensions={0} | all-to-all | bytes 524288 | tf_op jit(solution)/shard_map/all_to_all | solution.py:35
  279.6 0.7 convolution_subtract_fusion.2
  280.2 0.1 broadcast_in_dim.28
  280.4 31.6 %all_to_all.77 = f32[32,2,32,128]{3,2,1,0:T(8,128)S(1)} all-to-all(f32[32,2,32,128]{3,2,1,0:T(8,128)S(1)} %broadcast_in_dim.28), channel_id=1, replica_groups=mesh['dp_0'=8,'dp_1'=2,'dp_2'=2,'grp'=8] {'dp_0','dp_1','dp_2'}, dimensions={0} | all-to-all | bytes 2097152 | tf_op jit(solution)/shard_map/all_to_all | solution.py:35
  312.0 0.7 fusion.10
  312.7 12.0 %all_to_all.78 = f32[8,2,32,128]{3,2,1,0:T(8,128)S(1)} all-to-all(f32[8,2,32,128]{3,2,1,0:T(8,128)S(1)} %broadcast_in_dim.29), channel_id=1, replica_groups=mesh['dp_0'=8,'dp_1'=2,'dp_2'=2,'grp'=8] {'grp'}, dimensions={0} | all-to-all | bytes 524288 | tf_op jit(solution)/shard_map/all_to_all | solution.py:35
  324.7 0.7 convolution_subtract_fusion.1
  325.4 0.1 broadcast_in_dim.30
  325.5 31.6 %all_to_all.79 = f32[32,2,32,128]{3,2,1,0:T(8,128)S(1)} all-to-all(f32[32,2,32,128]{3,2,1,0:T(8,128)S(1)} %broadcast_in_dim.30), channel_id=1, replica_groups=mesh['dp_0'=8,'dp_1'=2,'dp_2'=2,'grp'=8] {'dp_0','dp_1','dp_2'}, dimensions={0} | all-to-all | bytes 2097152 | tf_op jit(solution)/shard_map/all_to_all | solution.py:35
  357.2 0.7 fusion.8
  357.9 12.1 %all_to_all.80 = f32[8,2,32,128]{3,2,1,0:T(8,128)S(1)} all-to-all(f32[8,2,32,128]{3,2,1,0:T(8,128)S(1)} %broadcast_in_dim.31), channel_id=1, replica_groups=mesh['dp_0'=8,'dp_1'=2,'dp_2'=2,'grp'=8] {'grp'}, dimensions={0} | all-to-all | bytes 524288 | tf_op jit(solution)/shard_map/all_to_all | solution.py:35
  370.0 0.7 convolution_subtract_fusion
  370.7 0.1 broadcast_in_dim.32
  370.8 31.7 %all_to_all.81 = f32[32,2,32,128]{3,2,1,0:T(8,128)S(1)} all-to-all(f32[32,2,32,128]{3,2,1,0:T(8,128)S(1)} %broadcast_in_dim.32), channel_id=1, replica_groups=mesh['dp_0'=8,'dp_1'=2,'dp_2'=2,'grp'=8] {'dp_0','dp_1','dp_2'}, dimensions={0} | all-to-all | bytes 2097152 | tf_op jit(solution)/shard_map/all_to_all | solution.py:35
  402.6 0.3 copy.48
  402.9 1.1 stack.15
  404.0 99.9 %all_to_all.82 = f32[8,2,1024,128]{2,3,1,0:T(8,128)S(1)} all-to-all(f32[8,2,1024,128]{2,3,1,0:T(8,128)S(1)} %stack.15), channel_id=1, replica_groups=mesh['dp_0'=8,'dp_1'=2,'dp_2'=2,'grp'=8] {'grp'}, dimensions={0} | all-to-all | bytes 16777216 | tf_op jit(solution)/shard_map/all_to_all | solution.py:16
  503.9 1.7 copy.95
  505.6 1.7 fusion.21
  507.2 3.5 fusion.22
  510.8 3.5 fusion.23
  514.2 7.1 %convolution_multiply_fusion = f32[1024,1024]{1,0:T(8,128)S(1)} fusion(f32[1024,512]{1,0:T(8,128)S(1)} %fusion.22, f32[1024,512]{1,0:T(8,128)S(1)} %fusion.23), kind=kOutput, calls=%fused_computation.2 | convolution fusion | flops 6443499520 | bytes 8388608 | tf_op jit(solution)/shard_map/dot_general | solution.py:119
  521.4 2.2 copy.50
  523.7 12.1 %reduce-scatter.6.cloned.1.call-done = f32[16,32,1024]{2,1,0:T(8,128)} async-done(((f32[32,32,1024]{2,1,0:T(8,128)}), f32[16,32,1024]{2,1,0:T(8,128)}) %reduce-scatter.6.cloned.1.call-update) | async-done | bytes 2097168 | tf_op jit(solution)/shard_map/reduce_scatter | solution.py:60
  535.8 79.4 %reduce-scatter.8.cloned.1.call-done = f32[1,32,1024]{2,1,0:T(8,128)} async-done(((f32[16,32,1024]{2,1,0:T(8,128)}), f32[1,32,1024]{2,1,0:T(8,128)}) %reduce-scatter.8.cloned.1.call-update) | async-done | bytes 131088 | tf_op jit(solution)/shard_map/reduce_scatter | solution.py:61
  615.2 0.9 copy.59
  616.2 13.1 %all_to_all.83 = f32[8,32,128]{2,1,0:T(8,128)S(1)} all-to-all(f32[8,32,128]{2,1,0:T(8,128)S(1)} %bitcast.132), channel_id=1, replica_groups=mesh['dp_0'=8,'dp_1'=2,'dp_2'=2,'grp'=8] {'grp'}, dimensions={0} | all-to-all | bytes 262144 | tf_op jit(solution)/shard_map/all_to_all | solution.py:29
  629.2 0.6 reduce_sum.29
  (31 shorter events, 0.9 us)
Async XLA Ops:
  6.5 2.9 copy-start
  6.5 142.8 %reduce-scatter.4.cloned.1.call-start = ((), (), s32[]{:S(2)}) async-start(), calls=%async_computation.17 | async-start | bytes 8650752 | tf_op jit(solution)/shard_map/reduce_scatter | solution.py:95
  15.0 150.1 %copy-start.2 = (f32[2]{0:T(128)S(1)}, f32[2]{0:T(128)}, u32[]{:S(2)}) copy-start(f32[2]{0:T(128)} %param.5) | copy-start | bytes 28
  151.0 14.0 %all-to-all-start = ((f32[8,2,32,128]{3,2,1,0:T(8,128)}), f32[8,2,32,128]{3,2,1,0:T(8,128)S(1)}, u32[]{:S(2)}, u32[]{:S(2)}) async-start(f32[8,2,32,128]{3,2,1,0:T(8,128)} %bitcast_bitcast_fusion), calls=%async_computation.1 | async-start | bytes 524288 | tf_op jit(solution)/shard_map/all_to_all | solution.py:29
  158.3 377.5 %reduce-scatter.6.cloned.1.call-start = ((), (), s32[]{:S(2)}) async-start(), calls=%async_computation.18 | async-start | bytes 6291456 | tf_op jit(solution)/shard_map/reduce_scatter | solution.py:60
  507.2 3.5 copy-start.1
  523.6 91.6 %reduce-scatter.8.cloned.1.call-start = ((), (), s32[]{:S(2)}) async-start(), calls=%async_computation.19 | async-start | bytes 2228224 | tf_op jit(solution)/shard_map/reduce_scatter | solution.py:61
Sparse Core Ops, SparseCore 0:
  15.1 134.1 reduce-scatter.3
  523.7 12.0 reduce-scatter.5
  538.3 76.8 reduce-scatter.7
